TPU v7x, 256 devices: a whole 4x4x8 slice. The times are simulated.
256 devices in a mesh: wide: 16 (over y_lo, x, core), narrow: 16 (over z, y_hi).
Axes of the slice: x: 4, y: 4 (y_hi: 2, y_lo: 2; y = y_hi * 2 + y_lo), z: 8, core: 2. Of those that a mesh axis runs over, the one named last changes fastest.
Arguments:
- right_side: bfloat16 [393216, 256], P(('wide', 'narrow')), may hold values from -6 to 6
- leaf_blocks: bfloat16 [393216, 1536], P(('wide', 'narrow')), may hold values from -8 to 16
- level_bases: bfloat16 [393216, 1024], P(('wide', 'narrow')), may hold values from -2 to 2
Outputs:
- solution_field: float32 [393216, 256], P(('wide', 'narrow'))
- residual: float32 [393216, 256], P(('wide', 'narrow'))
All inputs are finite; a program needn't handle non-finite values.
Results may differ from a plain program's by a relative error of at most 0.006.
Values may be sent and summed in bfloat16 or wider, within the bound.
A program may use at most 64 MiB of HBM per device.

v0:
```python
import jax
import jax.numpy as jnp
from jax import lax
from jax.sharding import PartitionSpec as P

ITERS = 2


centre = 6.0
half_width = 5.0


def partner_2(value, axis, distance):
    mask = 2**distance
    pairs = [(source, source ^ mask) for source in range(lax.axis_size(axis))]
    return lax.ppermute(value, axis, pairs)


def contract_rows(left, right):
    return lax.dot_general(
        left, right, (((0,), (0,)), ((), ())), preferred_element_type=jnp.float32
    )


def contract_last(left, right):
    return lax.dot_general(
        left, right, (((1,), (1,)), ((), ())), preferred_element_type=jnp.float32
    )


def pair_sum(values, bit_index, low_bits):
    if bit_index < low_bits:
        partner = partner_2(values, "narrow", bit_index)
    else:
        partner = partner_2(values, "wide", bit_index - low_bits)
    return values + partner


def sibling_of(values, bit_index, low_bits):
    if bit_index < low_bits:
        return partner_2(values, "narrow", bit_index)
    return partner_2(values, "wide", bit_index - low_bits)


def level_tree(projected, level_count, low_bits):
    block_width = projected.shape[1] // level_count
    results = []
    totals = projected
    for bit_index in range(level_count):
        offset = bit_index * block_width
        own = totals[:, offset : offset + block_width].astype(jnp.bfloat16)
        results.append(sibling_of(own, bit_index, low_bits))
        boundary = offset + block_width
        if boundary < level_count * block_width:
            summed = pair_sum(totals[:, boundary:], bit_index, low_bits)
            totals = jnp.concatenate([totals[:, :boundary], summed], axis=1)
    return results


def apply_kernel(operand, leaf_blocks, level_bases, low_bits, high_bits):
    leaf_part = jnp.dot(leaf_blocks, operand, preferred_element_type=jnp.float32)
    projected = contract_rows(operand, level_bases)
    siblings = jnp.concatenate(level_tree(projected, low_bits + high_bits, low_bits), axis=1)
    return leaf_part + contract_last(level_bases, siblings)


def on_device(right_side, leaf_blocks, level_bases):
    low_bits = lax.axis_size("narrow").bit_length() - 1
    high_bits = lax.axis_size("wide").bit_length() - 1
    residual = right_side.astype(jnp.float32)
    solution_field = jnp.zeros_like(residual)
    sigma_ratio = centre / half_width
    ratio_now = 1.0 / sigma_ratio
    direction = residual / centre
    for iteration in range(ITERS):
        solution_field = solution_field + direction
        applied = apply_kernel(
            direction.astype(jnp.bfloat16), leaf_blocks, level_bases, low_bits, high_bits
        )
        residual = residual - applied
        if iteration + 1 < ITERS:
            ratio_next = 1.0 / (2.0 * sigma_ratio - ratio_now)
            direction = (
                ratio_next * ratio_now * direction + 2.0 * ratio_next / half_width * residual
            )
            ratio_now = ratio_next
    return (solution_field, residual)


def solution(mesh):
    return jax.shard_map(
        on_device,
        mesh=mesh,
        in_specs=(
            P(("wide", "narrow"), None),
            P(("wide", "narrow"), None),
            P(("wide", "narrow"), None),
        ),
        out_specs=(P(("wide", "narrow"), None), P(("wide", "narrow"), None)),
        check_vma=False,
    )
```

profile of v0, /device:TPU:1, one launch (start us, length us, event | category | flops | bytes accessed | tf_op | source)
XLA Modules:
  0.0 281.2 jit_solution(1683725073214565039)
XLA Ops:
  5.3 3.8 %collective-permute-start.1 = (f32[256,896]{1,0:T(8,128)S(1)}, f32[256,896]{1,0:T(8,128)S(1)}, u32[]{:S(2)}, u32[]{:S(2)}) collective-permute-start(f32[256,896]{1,0:T(8,128)S(1)} %slice.127), channel_id=1, source_target_pairs={{0,1},{1,0},{2,3},{3,2},{4,5},{5,4},{6,7},{7,6},{8,9},{9,8},{10,11... | collective-permute-start | bytes 2752520 | tf_op jit(solution)/shard_map/ppermute | solution.py:16
  9.1 19.0 %collective-permute-done.1 = f32[256,896]{1,0:T(8,128)S(1)} collective-permute-done((f32[256,896]{1,0:T(8,128)S(1)}, f32[256,896]{1,0:T(8,128)S(1)}, u32[]{:S(2)}, u32[]{:S(2)}) %collective-permute-start.1) | collective-permute-done | bytes 917536 | tf_op jit(solution)/shard_map/ppermute | solution.py:16
  30.9 16.3 %collective-permute-done.3 = f32[256,768]{1,0:T(8,128)S(1)} collective-permute-done((f32[256,768]{1,0:T(8,128)S(1)}, f32[256,768]{1,0:T(8,128)S(1)}, u32[]{:S(2)}, u32[]{:S(2)}) %collective-permute-start.3) | collective-permute-done | bytes 786464 | tf_op jit(solution)/shard_map/ppermute | solution.py:16
  47.3 3.0 %collective-permute-start.5 = (f32[256,640]{1,0:T(8,128)S(1)}, f32[256,640]{1,0:T(8,128)S(1)}, u32[]{:S(2)}, u32[]{:S(2)}) collective-permute-start(f32[256,640]{1,0:T(8,128)S(1)} %slice.131), channel_id=1, source_target_pairs={{0,4},{1,5},{2,6},{3,7},{4,0},{5,1},{6,2},{7,3},{8,12},{9,13},{10,... | collective-permute-start | bytes 1966088 | tf_op jit(solution)/shard_map/ppermute | solution.py:16
  50.4 28.2 %collective-permute-done.5 = f32[256,640]{1,0:T(8,128)S(1)} collective-permute-done((f32[256,640]{1,0:T(8,128)S(1)}, f32[256,640]{1,0:T(8,128)S(1)}, u32[]{:S(2)}, u32[]{:S(2)}) %collective-permute-start.5) | collective-permute-done | bytes 655392 | tf_op jit(solution)/shard_map/ppermute | solution.py:16
  78.8 6.6 %collective-permute-start.7 = (f32[256,512]{1,0:T(8,128)S(1)}, f32[256,512]{1,0:T(8,128)S(1)}, u32[]{:S(2)}, u32[]{:S(2)}) collective-permute-start(f32[256,512]{1,0:T(8,128)S(1)} %slice.133), channel_id=1, source_target_pairs={{0,8},{1,9},{2,10},{3,11},{4,12},{5,13},{6,14},{7,15},{8,0},{9,1},... | collective-permute-start | bytes 1572872 | tf_op jit(solution)/shard_map/ppermute | solution.py:16
  85.3 3.0 %collective-permute-start = (bf16[256,128]{1,0:T(8,128)(2,1)S(1)}, bf16[256,128]{1,0:T(8,128)(2,1)S(1)}, u32[]{:S(2)}, u32[]{:S(2)}) collective-permute-start(bf16[256,128]{1,0:T(8,128)(2,1)S(1)} %slice.195), channel_id=1, source_target_pairs={{0,1},{1,0},{2,3},{3,2},{4,5},{5,4},{6,7},{7,6},{8,9},{9,8},{10,11... | collective-permute-start | bytes 196616 | tf_op jit(solution)/shard_map/ppermute | solution.py:16
  88.3 19.7 %collective-permute-done.7 = f32[256,512]{1,0:T(8,128)S(1)} collective-permute-done((f32[256,512]{1,0:T(8,128)S(1)}, f32[256,512]{1,0:T(8,128)S(1)}, u32[]{:S(2)}, u32[]{:S(2)}) %collective-permute-start.7) | collective-permute-done | bytes 524320 | tf_op jit(solution)/shard_map/ppermute | solution.py:16
  111.4 3.3 %collective-permute-start.4 = (bf16[256,128]{1,0:T(8,128)(2,1)S(1)}, bf16[256,128]{1,0:T(8,128)(2,1)S(1)}, u32[]{:S(2)}, u32[]{:S(2)}) collective-permute-start(bf16[256,128]{1,0:T(8,128)(2,1)S(1)} %slice.193), channel_id=1, source_target_pairs={{0,4},{1,5},{2,6},{3,7},{4,0},{5,1},{6,2},{7,3},{8,12},{9,13},{10,... | collective-permute-start | bytes 196616 | tf_op jit(solution)/shard_map/ppermute | solution.py:16
  118.6 4.7 %collective-permute-done.6 = bf16[256,128]{1,0:T(8,128)(2,1)S(1)} collective-permute-done((bf16[256,128]{1,0:T(8,128)(2,1)S(1)}, bf16[256,128]{1,0:T(8,128)(2,1)S(1)}, u32[]{:S(2)}, u32[]{:S(2)}) %collective-permute-start.6) | collective-permute-done | bytes 65568 | tf_op jit(solution)/shard_map/ppermute | solution.py:16
  129.4 2.8 %collective-permute-start.12 = (bf16[256,128]{1,0:T(8,128)(2,1)S(1)}, bf16[256,128]{1,0:T(8,128)(2,1)S(1)}, u32[]{:S(2)}, u32[]{:S(2)}) collective-permute-start(bf16[256,128]{1,0:T(8,128)(2,1)S(1)} %slice.189), channel_id=1, source_target_pairs={{0,64},{16,80},{32,96},{48,112},{64,0},{80,16},{96,32},{112,48},{1... | collective-permute-start | bytes 196616 | tf_op jit(solution)/shard_map/ppermute | solution.py:16
  141.1 3.0 %collective-permute-start.16 = (f32[256,896]{1,0:T(8,128)S(1)}, f32[256,896]{1,0:T(8,128)S(1)}, u32[]{:S(2)}, u32[]{:S(2)}) collective-permute-start(f32[256,896]{1,0:T(8,128)S(1)} %slice.141), channel_id=1, source_target_pairs={{0,1},{1,0},{2,3},{3,2},{4,5},{5,4},{6,7},{7,6},{8,9},{9,8},{10,11... | collective-permute-start | bytes 2752520 | tf_op jit(solution)/shard_map/ppermute | solution.py:16
  144.1 18.0 %collective-permute-done.16 = f32[256,896]{1,0:T(8,128)S(1)} collective-permute-done((f32[256,896]{1,0:T(8,128)S(1)}, f32[256,896]{1,0:T(8,128)S(1)}, u32[]{:S(2)}, u32[]{:S(2)}) %collective-permute-start.16) | collective-permute-done | bytes 917536 | tf_op jit(solution)/shard_map/ppermute | solution.py:16
  162.4 15.7 %collective-permute-done.18 = f32[256,768]{1,0:T(8,128)S(1)} collective-permute-done((f32[256,768]{1,0:T(8,128)S(1)}, f32[256,768]{1,0:T(8,128)S(1)}, u32[]{:S(2)}, u32[]{:S(2)}) %collective-permute-start.18) | collective-permute-done | bytes 786464 | tf_op jit(solution)/shard_map/ppermute | solution.py:16
  180.7 27.6 %collective-permute-done.20 = f32[256,640]{1,0:T(8,128)S(1)} collective-permute-done((f32[256,640]{1,0:T(8,128)S(1)}, f32[256,640]{1,0:T(8,128)S(1)}, u32[]{:S(2)}, u32[]{:S(2)}) %collective-permute-start.20) | collective-permute-done | bytes 655392 | tf_op jit(solution)/shard_map/ppermute | solution.py:16
  208.4 3.4 %collective-permute-start.22 = (f32[256,512]{1,0:T(8,128)S(1)}, f32[256,512]{1,0:T(8,128)S(1)}, u32[]{:S(2)}, u32[]{:S(2)}) collective-permute-start(f32[256,512]{1,0:T(8,128)S(1)} %slice.147), channel_id=1, source_target_pairs={{0,8},{1,9},{2,10},{3,11},{4,12},{5,13},{6,14},{7,15},{8,0},{9,1},... | collective-permute-start | bytes 1572872 | tf_op jit(solution)/shard_map/ppermute | solution.py:16
  212.4 2.9 %collective-permute-start.15 = (bf16[256,128]{1,0:T(8,128)(2,1)}, bf16[256,128]{1,0:T(8,128)(2,1)}, u32[]{:S(2)}, u32[]{:S(2)}) collective-permute-start(bf16[256,128]{1,0:T(8,128)(2,1)} %slice.188), channel_id=1, source_target_pairs={{0,1},{1,0},{2,3},{3,2},{4,5},{5,4},{6,7},{7,6},{8,9},{9,8},{10,11... | collective-permute-start | bytes 196616 | tf_op jit(solution)/shard_map/ppermute | solution.py:16
  215.4 21.9 %collective-permute-done.22 = f32[256,512]{1,0:T(8,128)S(1)} collective-permute-done((f32[256,512]{1,0:T(8,128)S(1)}, f32[256,512]{1,0:T(8,128)S(1)}, u32[]{:S(2)}, u32[]{:S(2)}) %collective-permute-start.22) | collective-permute-done | bytes 524320 | tf_op jit(solution)/shard_map/ppermute | solution.py:16
  241.6 3.0 %copy.6 = f32[1536,256]{1,0:T(8,128)} copy(f32[1536,256]{0,1:T(8,128)} %get-tuple-element.4) | data formatting | bytes 3145728
  247.3 4.1 %collective-permute-start.19 = (bf16[256,128]{1,0:T(8,128)(2,1)S(1)}, bf16[256,128]{1,0:T(8,128)(2,1)S(1)}, u32[]{:S(2)}, u32[]{:S(2)}) collective-permute-start(bf16[256,128]{1,0:T(8,128)(2,1)S(1)} %slice.186), channel_id=1, source_target_pairs={{0,4},{1,5},{2,6},{3,7},{4,0},{5,1},{6,2},{7,3},{8,12},{9,13},{10,... | collective-permute-start | bytes 196616 | tf_op jit(solution)/shard_map/ppermute | solution.py:16
  254.4 3.1 %collective-permute-start.21 = (bf16[256,128]{1,0:T(8,128)(2,1)S(1)}, bf16[256,128]{1,0:T(8,128)(2,1)S(1)}, u32[]{:S(2)}, u32[]{:S(2)}) collective-permute-start(bf16[256,128]{1,0:T(8,128)(2,1)S(1)} %slice.185), channel_id=1, source_target_pairs={{0,8},{1,9},{2,10},{3,11},{4,12},{5,13},{6,14},{7,15},{8,0},{9,1},... | collective-permute-start | bytes 196616 | tf_op jit(solution)/shard_map/ppermute | solution.py:16
  257.5 3.9 %collective-permute-done.21 = bf16[256,128]{1,0:T(8,128)(2,1)S(1)} collective-permute-done((bf16[256,128]{1,0:T(8,128)(2,1)S(1)}, bf16[256,128]{1,0:T(8,128)(2,1)S(1)}, u32[]{:S(2)}, u32[]{:S(2)}) %collective-permute-start.21) | collective-permute-done | bytes 65568 | tf_op jit(solution)/shard_map/ppermute | solution.py:16
  262.3 2.8 %collective-permute-start.23 = (bf16[256,128]{1,0:T(8,128)(2,1)S(1)}, bf16[256,128]{1,0:T(8,128)(2,1)S(1)}, u32[]{:S(2)}, u32[]{:S(2)}) collective-permute-start(bf16[256,128]{1,0:T(8,128)(2,1)S(1)} %slice.184), channel_id=1, source_target_pairs={{0,16},{16,0},{32,48},{48,32},{64,80},{80,64},{96,112},{112,96},{1... | collective-permute-start | bytes 196616 | tf_op jit(solution)/shard_map/ppermute | solution.py:16
  278.1 3.0 %copy.7 = f32[1536,256]{1,0:T(8,128)} copy(f32[1536,256]{0,1:T(8,128)} %fusion.2) | data formatting | bytes 3145728
  (126 shorter events, 57.0 us)
Async XLA Ops:
  5.3 22.9 %collective-permute-start.1 = (f32[256,896]{1,0:T(8,128)S(1)}, f32[256,896]{1,0:T(8,128)S(1)}, u32[]{:S(2)}, u32[]{:S(2)}) collective-permute-start(f32[256,896]{1,0:T(8,128)S(1)} %slice.127), channel_id=1, source_target_pairs={{0,1},{1,0},{2,3},{3,2},{4,5},{5,4},{6,7},{7,6},{8,9},{9,8},{10,11... | collective-permute-start | bytes 2752520 | tf_op jit(solution)/shard_map/ppermute | solution.py:16
  28.4 18.9 %collective-permute-start.3 = (f32[256,768]{1,0:T(8,128)S(1)}, f32[256,768]{1,0:T(8,128)S(1)}, u32[]{:S(2)}, u32[]{:S(2)}) collective-permute-start(f32[256,768]{1,0:T(8,128)S(1)} %slice.129), channel_id=1, source_target_pairs={{0,2},{1,3},{2,0},{3,1},{4,6},{5,7},{6,4},{7,5},{8,10},{9,11},{10,... | collective-permute-start | bytes 2359304 | tf_op jit(solution)/shard_map/ppermute | solution.py:16
  47.3 31.3 %collective-permute-start.5 = (f32[256,640]{1,0:T(8,128)S(1)}, f32[256,640]{1,0:T(8,128)S(1)}, u32[]{:S(2)}, u32[]{:S(2)}) collective-permute-start(f32[256,640]{1,0:T(8,128)S(1)} %slice.131), channel_id=1, source_target_pairs={{0,4},{1,5},{2,6},{3,7},{4,0},{5,1},{6,2},{7,3},{8,12},{9,13},{10,... | collective-permute-start | bytes 1966088 | tf_op jit(solution)/shard_map/ppermute | solution.py:16
  78.8 29.3 %collective-permute-start.7 = (f32[256,512]{1,0:T(8,128)S(1)}, f32[256,512]{1,0:T(8,128)S(1)}, u32[]{:S(2)}, u32[]{:S(2)}) collective-permute-start(f32[256,512]{1,0:T(8,128)S(1)} %slice.133), channel_id=1, source_target_pairs={{0,8},{1,9},{2,10},{3,11},{4,12},{5,13},{6,14},{7,15},{8,0},{9,1},... | collective-permute-start | bytes 1572872 | tf_op jit(solution)/shard_map/ppermute | solution.py:16
  85.3 25.9 %collective-permute-start = (bf16[256,128]{1,0:T(8,128)(2,1)S(1)}, bf16[256,128]{1,0:T(8,128)(2,1)S(1)}, u32[]{:S(2)}, u32[]{:S(2)}) collective-permute-start(bf16[256,128]{1,0:T(8,128)(2,1)S(1)} %slice.195), channel_id=1, source_target_pairs={{0,1},{1,0},{2,3},{3,2},{4,5},{5,4},{6,7},{7,6},{8,9},{9,8},{10,11... | collective-permute-start | bytes 196616 | tf_op jit(solution)/shard_map/ppermute | solution.py:16
  108.1 6.6 %collective-permute-start.9 = (f32[256,384]{1,0:T(8,128)S(1)}, f32[256,384]{1,0:T(8,128)S(1)}, u32[]{:S(2)}, u32[]{:S(2)}) collective-permute-start(f32[256,384]{1,0:T(8,128)S(1)} %slice.135), channel_id=1, source_target_pairs={{0,16},{16,0},{32,48},{48,32},{64,80},{80,64},{96,112},{112,96},{1... | collective-permute-start | bytes 1179656 | tf_op jit(solution)/shard_map/ppermute | solution.py:16
  111.4 7.1 %collective-permute-start.4 = (bf16[256,128]{1,0:T(8,128)(2,1)S(1)}, bf16[256,128]{1,0:T(8,128)(2,1)S(1)}, u32[]{:S(2)}, u32[]{:S(2)}) collective-permute-start(bf16[256,128]{1,0:T(8,128)(2,1)S(1)} %slice.193), channel_id=1, source_target_pairs={{0,4},{1,5},{2,6},{3,7},{4,0},{5,1},{6,2},{7,3},{8,12},{9,13},{10,... | collective-permute-start | bytes 196616 | tf_op jit(solution)/shard_map/ppermute | solution.py:16
  114.8 11.7 %collective-permute-start.11 = (f32[256,256]{1,0:T(8,128)S(1)}, f32[256,256]{1,0:T(8,128)S(1)}, u32[]{:S(2)}, u32[]{:S(2)}) collective-permute-start(f32[256,256]{1,0:T(8,128)S(1)} %slice.137), channel_id=1, source_target_pairs={{0,32},{16,48},{32,0},{48,16},{64,96},{80,112},{96,64},{112,80},{1... | collective-permute-start | bytes 786440 | tf_op jit(solution)/shard_map/ppermute | solution.py:16
  116.2 7.1 %collective-permute-start.6 = (bf16[256,128]{1,0:T(8,128)(2,1)S(1)}, bf16[256,128]{1,0:T(8,128)(2,1)S(1)}, u32[]{:S(2)}, u32[]{:S(2)}) collective-permute-start(bf16[256,128]{1,0:T(8,128)(2,1)S(1)} %slice.192), channel_id=1, source_target_pairs={{0,8},{1,9},{2,10},{3,11},{4,12},{5,13},{6,14},{7,15},{8,0},{9,1},... | collective-permute-start | bytes 196616 | tf_op jit(solution)/shard_map/ppermute | solution.py:16
  123.4 5.9 %collective-permute-start.8 = (bf16[256,128]{1,0:T(8,128)(2,1)S(1)}, bf16[256,128]{1,0:T(8,128)(2,1)S(1)}, u32[]{:S(2)}, u32[]{:S(2)}) collective-permute-start(bf16[256,128]{1,0:T(8,128)(2,1)S(1)} %slice.191), channel_id=1, source_target_pairs={{0,16},{16,0},{32,48},{48,32},{64,80},{80,64},{96,112},{112,96},{1... | collective-permute-start | bytes 196616 | tf_op jit(solution)/shard_map/ppermute | solution.py:16
  126.5 7.6 %collective-permute-start.13 = (f32[256,128]{1,0:T(8,128)S(1)}, f32[256,128]{1,0:T(8,128)S(1)}, u32[]{:S(2)}, u32[]{:S(2)}) collective-permute-start(f32[256,128]{1,0:T(8,128)S(1)} %slice.139), channel_id=1, source_target_pairs={{0,64},{16,80},{32,96},{48,112},{64,0},{80,16},{96,32},{112,48},{1... | collective-permute-start | bytes 393224 | tf_op jit(solution)/shard_map/ppermute | solution.py:16
  129.4 6.3 %collective-permute-start.12 = (bf16[256,128]{1,0:T(8,128)(2,1)S(1)}, bf16[256,128]{1,0:T(8,128)(2,1)S(1)}, u32[]{:S(2)}, u32[]{:S(2)}) collective-permute-start(bf16[256,128]{1,0:T(8,128)(2,1)S(1)} %slice.189), channel_id=1, source_target_pairs={{0,64},{16,80},{32,96},{48,112},{64,0},{80,16},{96,32},{112,48},{1... | collective-permute-start | bytes 196616 | tf_op jit(solution)/shard_map/ppermute | solution.py:16
  141.1 21.0 %collective-permute-start.16 = (f32[256,896]{1,0:T(8,128)S(1)}, f32[256,896]{1,0:T(8,128)S(1)}, u32[]{:S(2)}, u32[]{:S(2)}) collective-permute-start(f32[256,896]{1,0:T(8,128)S(1)} %slice.141), channel_id=1, source_target_pairs={{0,1},{1,0},{2,3},{3,2},{4,5},{5,4},{6,7},{7,6},{8,9},{9,8},{10,11... | collective-permute-start | bytes 2752520 | tf_op jit(solution)/shard_map/ppermute | solution.py:16
  162.3 15.8 %collective-permute-start.18 = (f32[256,768]{1,0:T(8,128)S(1)}, f32[256,768]{1,0:T(8,128)S(1)}, u32[]{:S(2)}, u32[]{:S(2)}) collective-permute-start(f32[256,768]{1,0:T(8,128)S(1)} %slice.143), channel_id=1, source_target_pairs={{0,2},{1,3},{2,0},{3,1},{4,6},{5,7},{6,4},{7,5},{8,10},{9,11},{10,... | collective-permute-start | bytes 2359304 | tf_op jit(solution)/shard_map/ppermute | solution.py:16
  178.3 30.0 %collective-permute-start.20 = (f32[256,640]{1,0:T(8,128)S(1)}, f32[256,640]{1,0:T(8,128)S(1)}, u32[]{:S(2)}, u32[]{:S(2)}) collective-permute-start(f32[256,640]{1,0:T(8,128)S(1)} %slice.145), channel_id=1, source_target_pairs={{0,4},{1,5},{2,6},{3,7},{4,0},{5,1},{6,2},{7,3},{8,12},{9,13},{10,... | collective-permute-start | bytes 1966088 | tf_op jit(solution)/shard_map/ppermute | solution.py:16
  208.4 28.9 %collective-permute-start.22 = (f32[256,512]{1,0:T(8,128)S(1)}, f32[256,512]{1,0:T(8,128)S(1)}, u32[]{:S(2)}, u32[]{:S(2)}) collective-permute-start(f32[256,512]{1,0:T(8,128)S(1)} %slice.147), channel_id=1, source_target_pairs={{0,8},{1,9},{2,10},{3,11},{4,12},{5,13},{6,14},{7,15},{8,0},{9,1},... | collective-permute-start | bytes 1572872 | tf_op jit(solution)/shard_map/ppermute | solution.py:16
  212.4 32.2 %collective-permute-start.15 = (bf16[256,128]{1,0:T(8,128)(2,1)}, bf16[256,128]{1,0:T(8,128)(2,1)}, u32[]{:S(2)}, u32[]{:S(2)}) collective-permute-start(bf16[256,128]{1,0:T(8,128)(2,1)} %slice.188), channel_id=1, source_target_pairs={{0,1},{1,0},{2,3},{3,2},{4,5},{5,4},{6,7},{7,6},{8,9},{9,8},{10,11... | collective-permute-start | bytes 196616 | tf_op jit(solution)/shard_map/ppermute | solution.py:16
  238.2 13.2 %collective-permute-start.24 = (f32[256,384]{1,0:T(8,128)S(1)}, f32[256,384]{1,0:T(8,128)}, u32[]{:S(2)}, u32[]{:S(2)}) collective-permute-start(f32[256,384]{1,0:T(8,128)S(1)} %slice.149), channel_id=1, source_target_pairs={{0,16},{16,0},{32,48},{48,32},{64,80},{80,64},{96,112},{112,96},{1... | collective-permute-start | bytes 1179656 | tf_op jit(solution)/shard_map/ppermute | solution.py:16
  246.4 7.0 %collective-permute-start.17 = (bf16[256,128]{1,0:T(8,128)(2,1)S(1)}, bf16[256,128]{1,0:T(8,128)(2,1)S(1)}, u32[]{:S(2)}, u32[]{:S(2)}) collective-permute-start(bf16[256,128]{1,0:T(8,128)(2,1)S(1)} %slice.187), channel_id=1, source_target_pairs={{0,2},{1,3},{2,0},{3,1},{4,6},{5,7},{6,4},{7,5},{8,10},{9,11},{10,... | collective-permute-start | bytes 196616 | tf_op jit(solution)/shard_map/ppermute | solution.py:16
  247.3 10.2 %collective-permute-start.19 = (bf16[256,128]{1,0:T(8,128)(2,1)S(1)}, bf16[256,128]{1,0:T(8,128)(2,1)S(1)}, u32[]{:S(2)}, u32[]{:S(2)}) collective-permute-start(bf16[256,128]{1,0:T(8,128)(2,1)S(1)} %slice.186), channel_id=1, source_target_pairs={{0,4},{1,5},{2,6},{3,7},{4,0},{5,1},{6,2},{7,3},{8,12},{9,13},{10,... | collective-permute-start | bytes 196616 | tf_op jit(solution)/shard_map/ppermute | solution.py:16
  252.6 13.5 %collective-permute-start.26 = (f32[256,256]{1,0:T(8,128)S(1)}, f32[256,256]{1,0:T(8,128)S(1)}, u32[]{:S(2)}, u32[]{:S(2)}) collective-permute-start(f32[256,256]{1,0:T(8,128)S(1)} %slice.151), channel_id=1, source_target_pairs={{0,32},{16,48},{32,0},{48,16},{64,96},{80,112},{96,64},{112,80},{1... | collective-permute-start | bytes 786440 | tf_op jit(solution)/shard_map/ppermute | solution.py:16
  254.4 7.0 %collective-permute-start.21 = (bf16[256,128]{1,0:T(8,128)(2,1)S(1)}, bf16[256,128]{1,0:T(8,128)(2,1)S(1)}, u32[]{:S(2)}, u32[]{:S(2)}) collective-permute-start(bf16[256,128]{1,0:T(8,128)(2,1)S(1)} %slice.185), channel_id=1, source_target_pairs={{0,8},{1,9},{2,10},{3,11},{4,12},{5,13},{6,14},{7,15},{8,0},{9,1},... | collective-permute-start | bytes 196616 | tf_op jit(solution)/shard_map/ppermute | solution.py:16
  262.3 5.6 %collective-permute-start.23 = (bf16[256,128]{1,0:T(8,128)(2,1)S(1)}, bf16[256,128]{1,0:T(8,128)(2,1)S(1)}, u32[]{:S(2)}, u32[]{:S(2)}) collective-permute-start(bf16[256,128]{1,0:T(8,128)(2,1)S(1)} %slice.184), channel_id=1, source_target_pairs={{0,16},{16,0},{32,48},{48,32},{64,80},{80,64},{96,112},{112,96},{1... | collective-permute-start | bytes 196616 | tf_op jit(solution)/shard_map/ppermute | solution.py:16
  266.1 6.5 %collective-permute-start.28 = (f32[256,128]{1,0:T(8,128)S(1)}, f32[256,128]{1,0:T(8,128)S(1)}, u32[]{:S(2)}, u32[]{:S(2)}) collective-permute-start(f32[256,128]{1,0:T(8,128)S(1)} %slice.153), channel_id=1, source_target_pairs={{0,64},{16,80},{32,96},{48,112},{64,0},{80,16},{96,32},{112,48},{1... | collective-permute-start | bytes 393224 | tf_op jit(solution)/shard_map/ppermute | solution.py:16
  (17 other events, 465.8 us)
where the time goes:
time: 282 us; the launch traced here: 281 us
  waiting for transfers between devices  183 us (65%)
  starting transfers between devices  67.5 us (24%)
  local copies, waits for them, and re-layouts  15.5 us (5%)
  matrix products  11.9 us (4%)
    ppermute x30, waiting for transfers between devices, partner_2(): return lax.ppermute(value, axis, pairs)  183 us
    ppermute x30, starting transfers between devices, partner_2(): return lax.ppermute(value, axis, pairs)  67.5 us
    unnamed x39, local copies, waits for them, and re-layouts  10.4 us
  transfers between devices with their start and end apart: 30, of which 16 were waited for; matrix products, arithmetic and copies ran while one was open for 5% of the time, Pallas kernels for 0%

commit v1 on v0

v1 whole, which is shorter than its diff:
```python
import jax
import jax.numpy as jnp
from jax import lax
from jax.experimental import pallas as pl
from jax.experimental.pallas import tpu as pltpu
from jax.sharding import PartitionSpec as P

MESH = pl.DeviceIdType.MESH
F32, BF16 = jnp.float32, jnp.bfloat16
LEAF, RANK, VECS, LEVELS, ITERS = 1536, 128, 256, 8, 2
CENTRE, HALF = 6.0, 5.0
CH = 256
NCH = LEAF // CH
SIGMA = CENTRE / HALF
Q0 = 1.0 / SIGMA
Q1 = 1.0 / (2.0 * SIGMA - Q0)
KEEP, GAIN = Q1 * Q0, 2.0 * Q1 / HALF
S0, S1, S2, S3, SH, R1, R2, R3, RH, WH = range(10)


def flip(v, bit):
    return v + bit - 2 * bit * ((v // bit) % 2)


def kernel(
    r_hbm, l_hbm, b_hbm, x_hbm, o_hbm,
    r_v, l_v, b_v, d_v, acc_v, x_v, pacc, proj, sib, st,
    r1, r2, r3, rh, q1, q2, q3, qh, wv, tv,
    in_sem, out_sem, send_sem, recv_sem,
):
    w = lax.axis_index("wide")
    n = lax.axis_index("narrow")
    yl, x, c = w // 8, (w // 2) % 4, w % 2
    z, yh = n // 2, n % 2
    oyl = 1 - yl

    def dev(yl_, x_, c_, z_, yh_):
        return {"wide": yl_ * 8 + x_ * 2 + c_, "narrow": z_ * 2 + yh_}

    def rows(i, size):
        return pl.ds(pl.multiple_of(i * size, size), size)

    def send(src, dst, t, group, to):
        pltpu.make_async_remote_copy(
            src_ref=src, dst_ref=dst, send_sem=send_sem.at[t, group],
            recv_sem=recv_sem.at[t, group], device_id=to, device_id_type=MESH,
        ).start()

    def wait(ref, sem):
        pltpu.make_async_copy(ref, ref, sem).wait()

    pltpu.make_async_copy(r_hbm, r_v, in_sem.at[0]).start()
    for i in range(NCH):
        part = pl.ds(i * CH, CH)
        pltpu.make_async_copy(b_hbm.at[part], b_v.at[part], in_sem.at[1 + i]).start()
    for i in range(NCH):
        part = pl.ds(i * CH, CH)
        pltpu.make_async_copy(l_hbm.at[part], l_v.at[part], in_sem.at[1 + NCH + i]).start()

    barrier = pltpu.get_barrier_semaphore()

    def greet(to):
        pl.semaphore_signal(barrier, inc=1, device_id=to, device_id_type=MESH)

    def greet_ring(i, carry):
        for h in range(2):
            greet(dev(oyl, x, c, i, h))
        return carry

    lax.fori_loop(0, 8, greet_ring, 0)
    greet(dev(yl, x, c, z, 1 - yh))
    greet(dev(yl, x, 1 - c, z, yh))
    for dx in range(1, 4):
        for cc in range(2):
            greet(dev(yl, (x + dx) % 4, cc, z, yh))
    for dx in range(1, 4):
        for cc in range(2):
            greet(dev(oyl, (x + dx) % 4, cc, z, yh))
    greet(dev(oyl, x, 1 - c, z, yh))

    def project(k, first):
        part = rows(k, CH)
        p = lax.dot_general(
            d_v[part, :], b_v[part, :], (((0,), (0,)), ((), ())),
            preferred_element_type=F32,
        )
        if first:
            pacc[...] = p
        else:
            pacc[...] += p

    def scatter(t):
        for k in range(LEVELS):
            proj[t, k] = pacc[:, k * RANK:(k + 1) * RANK].astype(BF16)
        if t == 0:
            pl.semaphore_wait(barrier, 31)

        def ring(i, carry):
            step = jnp.where(i == 7, 0, jnp.where(i % 2 == 0, 4 + i // 2, 3 - i // 2))
            zz = (z + step) % 8
            for h in range(2):
                hh = (yh + 1 - h) % 2
                send(
                    proj.at[t, pl.ds(4, 4), rows(zz * 2 + hh, 16)], rh.at[t, n],
                    t, RH, dev(oyl, x, c, zz, hh),
                )
            return carry

        lax.fori_loop(0, 8, ring, 0)
        for a in range(4):
            zz = (z // 4) * 4 + (z % 4 + 3 - a + 4) % 4
            for h in range(2):
                send(
                    proj.at[t, 3, rows((zz % 4) * 2 + h, 32)],
                    r3.at[t, (z % 4) * 2 + yh], t, R3, dev(oyl, x, c, zz, h),
                )
        for a in range(2):
            zz = (z // 2) * 2 + (z % 2 + 1 - a) % 2
            for h in range(2):
                send(
                    proj.at[t, 2, rows((zz % 2) * 2 + h, 64)],
                    r2.at[t, (z % 2) * 2 + yh], t, R2, dev(oyl, x, c, zz, h),
                )
        for h in range(2):
            send(proj.at[t, 1, pl.ds(h * 128, 128)], r1.at[t, yh], t, R1, dev(oyl, x, c, z, h))
        send(proj.at[t, 0], sib.at[t, 0], t, S0, dev(yl, x, c, z, 1 - yh))

    def high_wide(t):
        wait(rh.at[t], recv_sem.at[t, RH])
        for k in range(4):
            total = rh[t, 0, k].astype(F32)
            for i in range(1, 16):
                total = total + rh[t, i, k].astype(F32)
            qh[t, k] = total.astype(BF16)
        for dx in range(3, -1, -1):
            for cc in range(2):
                send(qh.at[t, 3], wv.at[t, 7 + x * 2 + c], t, WH, dev(oyl, (x + dx) % 4, cc, z, yh))
        for a in range(2):
            xx = (flip(x, 2) // 2) * 2 + a
            for cc in range(2):
                send(qh.at[t, 2], wv.at[t, 3 + (x % 2) * 2 + c], t, WH, dev(yl, xx, cc, z, yh))
        for cc in range(2):
            send(qh.at[t, 1], wv.at[t, 1 + c], t, WH, dev(yl, flip(x, 1), cc, z, yh))
        send(qh.at[t, 0], wv.at[t, 0], t, WH, dev(yl, x, 1 - c, z, yh))

    def high_spread(t):
        wait(wv.at[t], recv_sem.at[t, WH])
        tv[t, 0] = wv[t, 0]
        tv[t, 1] = (wv[t, 1].astype(F32) + wv[t, 2].astype(F32)).astype(BF16)
        total = wv[t, 3].astype(F32)
        for i in range(4, 7):
            total = total + wv[t, i].astype(F32)
        tv[t, 2] = total.astype(BF16)
        total = wv[t, 7].astype(F32)
        for i in range(8, 15):
            total = total + wv[t, i].astype(F32)
        tv[t, 3] = total.astype(BF16)

        def ring(i, carry):
            step = jnp.where(i == 7, 0, jnp.where(i % 2 == 0, 4 + i // 2, 3 - i // 2))
            zz = (z + step) % 8
            for h in range(2):
                send(
                    tv.at[t], sib.at[t, pl.ds(4, 4), rows(n, 16)],
                    t, SH, dev(oyl, x, c, zz, h),
                )
            return carry

        lax.fori_loop(0, 8, ring, 0)

    def low(t):
        wait(r1.at[t], recv_sem.at[t, R1])
        q1[t] = (r1[t, 0].astype(F32) + r1[t, 1].astype(F32)).astype(BF16)
        for h in range(2):
            send(q1.at[t], sib.at[t, 1, rows(yh, 128)], t, S1, dev(oyl, x, c, flip(z, 1), h))
        wait(r2.at[t], recv_sem.at[t, R2])
        total = r2[t, 0].astype(F32)
        for i in range(1, 4):
            total = total + r2[t, i].astype(F32)
        q2[t] = total.astype(BF16)
        for a in range(2):
            zz = (flip(z, 2) // 2) * 2 + a
            for h in range(2):
                send(q2.at[t], sib.at[t, 2, rows((z % 2) * 2 + yh, 64)], t, S2, dev(oyl, x, c, zz, h))
        wait(r3.at[t], recv_sem.at[t, R3])
        total = r3[t, 0].astype(F32)
        for i in range(1, 8):
            total = total + r3[t, i].astype(F32)
        q3[t] = total.astype(BF16)
        for a in range(4):
            zz = (1 - z // 4) * 4 + a
            for h in range(2):
                send(q3.at[t], sib.at[t, 3, rows((z % 4) * 2 + yh, 32)], t, S3, dev(oyl, x, c, zz, h))

    def leaf(k, load):
        part = rows(k, CH)
        return jnp.dot(l_v[part, :], d_v[...], preferred_element_type=F32)

    wait(r_v, in_sem.at[0])
    d_v[...] = (r_v[...].astype(F32) / CENTRE).astype(BF16)
    for k in range(NCH):
        part = pl.ds(k * CH, CH)
        wait(b_v.at[part], in_sem.at[1 + k])
        project(k, k == 0)
    scatter(0)
    for k in range(NCH):
        part = pl.ds(k * CH, CH)
        wait(l_v.at[part], in_sem.at[1 + NCH + k])

    def leaf_0(k, carry):
        part = rows(k, CH)
        acc_v[part, :] = r_v[part, :].astype(F32) - leaf(k, True)
        return carry

    lax.fori_loop(0, NCH, leaf_0, 0)
    high_wide(0)
    low(0)
    high_spread(0)

    def gather_low(t):
        for k, s in ((0, S0), (1, S1), (2, S2), (3, S3)):
            wait(sib.at[t, k], recv_sem.at[t, s])
            st[k * RANK:(k + 1) * RANK, :] = sib[t, k].T

    def gather_high(t):
        wait(sib.at[t, pl.ds(4, 4)], recv_sem.at[t, SH])
        for k in range(4, LEVELS):
            st[k * RANK:(k + 1) * RANK, :] = sib[t, k].T

    def expand_low(k, carry):
        part = rows(k, CH)
        acc_v[part, :] -= jnp.dot(
            b_v[part, 0:4 * RANK], st[0:4 * RANK, :], preferred_element_type=F32
        )
        return carry

    def expand_high(k):
        part = rows(k, CH)
        return acc_v[part, :] - jnp.dot(
            b_v[part, 4 * RANK:], st[4 * RANK:, :], preferred_element_type=F32
        )

    gather_low(0)
    lax.fori_loop(0, NCH, expand_low, 0)
    gather_high(0)
    pacc[...] = jnp.zeros_like(pacc)

    def middle(k, carry):
        part = rows(k, CH)
        residual = expand_high(k)
        d0 = r_v[part, :].astype(F32) / CENTRE
        d1 = KEEP * d0 + GAIN * residual
        acc_v[part, :] = residual
        x_v[part, :] = d0 + d1
        d_v[part, :] = d1.astype(BF16)
        project(k, False)
        return carry

    lax.fori_loop(0, NCH, middle, 0)
    scatter(1)
    pltpu.make_async_copy(x_v, x_hbm, out_sem.at[0]).start()

    def leaf_1(k, carry):
        part = rows(k, CH)
        acc_v[part, :] -= leaf(k, False)
        return carry

    lax.fori_loop(0, NCH, leaf_1, 0)
    high_wide(1)
    low(1)
    high_spread(1)
    gather_low(1)
    lax.fori_loop(0, NCH, expand_low, 0)
    gather_high(1)
    for k in range(NCH):
        part = pl.ds(k * CH, CH)
        acc_v[part, :] = expand_high(k)
        pltpu.make_async_copy(acc_v.at[part], o_hbm.at[part], out_sem.at[1 + k]).start()

    for t in range(ITERS):
        for k, s in ((0, S0), (1, R1), (2, R2), (3, R3), (1, S1), (2, S2), (3, S3)):
            wait(proj.at[t, k], send_sem.at[t, s])
        for s in (RH, SH):
            wait(proj.at[t, pl.ds(4, 4)], send_sem.at[t, s])
        wait(wv.at[t], send_sem.at[t, WH])
    wait(x_v, out_sem.at[0])
    for k in range(NCH):
        part = pl.ds(k * CH, CH)
        wait(acc_v.at[part], out_sem.at[1 + k])


def on_device(right_side, leaf_blocks, level_bases):
    any_space = pl.BlockSpec(memory_space=pl.ANY)
    out = jax.ShapeDtypeStruct((LEAF, VECS), F32)
    return pl.pallas_call(
        kernel,
        out_shape=(out, out),
        in_specs=[any_space] * 3,
        out_specs=(any_space, any_space),
        scratch_shapes=[
            pltpu.VMEM((LEAF, VECS), BF16),
            pltpu.VMEM((LEAF, LEAF), BF16),
            pltpu.VMEM((LEAF, LEVELS * RANK), BF16),
            pltpu.VMEM((LEAF, VECS), BF16),
            pltpu.VMEM((LEAF, VECS), F32),
            pltpu.VMEM((LEAF, VECS), F32),
            pltpu.VMEM((VECS, LEVELS * RANK), F32),
            pltpu.VMEM((ITERS, LEVELS, VECS, RANK), BF16),
            pltpu.VMEM((ITERS, LEVELS, VECS, RANK), BF16),
            pltpu.VMEM((LEVELS * RANK, VECS), BF16),
            pltpu.VMEM((ITERS, 2, 128, RANK), BF16),
            pltpu.VMEM((ITERS, 4, 64, RANK), BF16),
            pltpu.VMEM((ITERS, 8, 32, RANK), BF16),
            pltpu.VMEM((ITERS, 16, 4, 16, RANK), BF16),
            pltpu.VMEM((ITERS, 128, RANK), BF16),
            pltpu.VMEM((ITERS, 64, RANK), BF16),
            pltpu.VMEM((ITERS, 32, RANK), BF16),
            pltpu.VMEM((ITERS, 4, 16, RANK), BF16),
            pltpu.VMEM((ITERS, 15, 16, RANK), BF16),
            pltpu.VMEM((ITERS, 4, 16, RANK), BF16),
            pltpu.SemaphoreType.DMA((1 + 2 * NCH,)),
            pltpu.SemaphoreType.DMA((1 + NCH,)),
            pltpu.SemaphoreType.DMA((ITERS, 10)),
            pltpu.SemaphoreType.DMA((ITERS, 10)),
        ],
        compiler_params=pltpu.CompilerParams(
            collective_id=0, has_side_effects=True, vmem_limit_bytes=48 * 1024 * 1024
        ),
        name="chebyshev",
    )(right_side, leaf_blocks, level_bases)


def solution(mesh):
    return jax.shard_map(
        on_device,
        mesh=mesh,
        in_specs=(P(("wide", "narrow"), None),) * 3,
        out_specs=(P(("wide", "narrow"), None),) * 2,
        check_vma=False,
    )
```

time: 282 us -> 65.7 us (0.23)
  waiting for transfers between devices: 183 us -> 0 us
  starting transfers between devices: 67.5 us -> 0 us
  Pallas kernels: 0 us -> 61.5 us
  local copies, waits for them, and re-layouts: 15.5 us -> 3.41 us
  matrix products: 11.9 us -> 0 us
    ppermute x30 -> x0, waiting for transfers between devices: 183 us -> none  [partner_2(): return lax.ppermute(value, axis, pairs)]
    ppermute x30 -> x0, starting transfers between devices: 67.5 us -> none  [partner_2(): return lax.ppermute(value, axis, pairs)]
    pallas_call x0 -> x1, Pallas kernels: none -> 61.5 us  [on_device(): pl.pallas_call(kernel, out_shape=(out, out), in_specs=[any_space] * 3, ou...]
    dot_general x6 -> x0, matrix products: 11.9 us -> none  [the longest x2 4.8 us: contract_last(): lax.dot_general(left, right, (((1,), (1,)), ((), ())), preferred_element_...]
    unnamed x39 -> x4, local copies, waits for them, and re-layouts: 10.4 us -> 3.41 us
    slice x28 -> x0, local copies, waits for them, and re-layouts: 5.03 us -> none  [the longest x14 4.45 us: level_tree(): own = totals[:, offset:offset + block_width].astype(jnp.bfloat16)]
  transfers between devices with their start and end apart: 30 -> 0, of which waited for: 16 -> 0; matrix products, arithmetic and copies ran while one was open for 5% -> 0% of each run, Pallas kernels for 0% -> 0%
where the time goes in v1:
time: 65.7 us; the launch traced here: 65.6 us
  Pallas kernels  61.5 us (94%)
  local copies, waits for them, and re-layouts  3.41 us (5%)
    pallas_call x1, Pallas kernels, on_device(): pl.pallas_call(kernel, out_shape=(out, out), in_specs=[any_space] * 3, ou...  61.5 us
    unnamed x4, local copies, waits for them, and re-layouts  3.41 us

profile of v1, /device:TPU:1, one launch (start us, length us, event | category | flops | bytes accessed | tf_op | source)
XLA Modules:
  0.0 65.6 jit_solution(3885478488759620738)
XLA Ops:
  0.6 0.0 copy-start
  0.6 1.1 %copy-done = bf16[1536,256]{1,0:T(8,128)(2,1)S(1)} copy-done((bf16[1536,256]{1,0:T(8,128)(2,1)S(1)}, bf16[1536,256]{1,0:T(8,128)(2,1)}, u32[]{:S(2)}) %copy-start) | copy-done | bytes 786456
  1.8 61.5 %chebyshev.1 = (f32[1536,256]{1,0:T(8,128)S(1)}, f32[1536,256]{1,0:T(8,128)S(1)}) custom-call(bf16[1536,256]{1,0:T(8,128)(2,1)S(1)} %copy-done, bf16[1536,1536]{1,0:T(8,128)(2,1)} %l_hbm.1, bf16[1536,1024]{1,0:T(8,128)(2,1)} %b_hbm.1), custom_call_target="tpu_custom_call" | custom-call | tf_op jit(solution)/shard_map/chebyshev/pallas_call | solution.py:295
  63.3 1.1 %copy.7 = f32[1536,256]{1,0:T(8,128)} copy(f32[1536,256]{1,0:T(8,128)S(1)} %get-tuple-element.4) | data formatting | bytes 3145728
  64.4 1.1 %copy.8 = f32[1536,256]{1,0:T(8,128)} copy(f32[1536,256]{1,0:T(8,128)S(1)} %get-tuple-element.5) | data formatting | bytes 3145728
Async XLA Ops:
  0.6 1.1 %copy-start = (bf16[1536,256]{1,0:T(8,128)(2,1)S(1)}, bf16[1536,256]{1,0:T(8,128)(2,1)}, u32[]{:S(2)}) copy-start(bf16[1536,256]{1,0:T(8,128)(2,1)} %r_hbm.1) | copy-start | bytes 2359300

commit v2 on v1

v2 whole, which is shorter than its diff:
```python
import jax
import jax.numpy as jnp
from jax import lax
from jax.experimental import pallas as pl
from jax.experimental.pallas import tpu as pltpu
from jax.sharding import PartitionSpec as P

MESH = pl.DeviceIdType.MESH
F32, BF16 = jnp.float32, jnp.bfloat16
LEAF, RANK, VECS, LEVELS, ITERS = 1536, 128, 256, 8, 2
COLS = LEVELS * RANK
HIGH = 4 * RANK
CENTRE, HALF = 6.0, 5.0
CH = 256
NCH = LEAF // CH
BIG = 512
NBIG = LEAF // BIG
SIGMA = CENTRE / HALF
Q0 = 1.0 / SIGMA
Q1 = 1.0 / (2.0 * SIGMA - Q0)
KEEP, GAIN = Q1 * Q0, 2.0 * Q1 / HALF
S0, S1, S2, S3, S4, S5, S67, R0, R1, R2, R3, RH, D5, P1, P6, P7 = range(16)
PEERS = 52


def flip(v, bit):
    return v + bit - 2 * bit * ((v // bit) % 2)


def kernel(
    r_hbm, l_hbm, b_hbm,
    acc_v, x_v, b_v, st,
    r_v, l_v, d_v, u_v, pacc, gacc, gram, proj, sib,
    r0, r1, r2, r3, rh, d5, p1, w6, w7, q1, q2, q3, q45, t4, t5, qp, tp,
    in_sem, send_sem, recv_sem,
):
    w = lax.axis_index("wide")
    n = lax.axis_index("narrow")
    yl, x, c = w // 8, (w // 2) % 4, w % 2
    z, yh = n // 2, n % 2
    oyl = 1 - yl
    plane = x * 4 + c * 2 + yh

    def dev(yl_, x_, c_, z_, yh_):
        return {"wide": yl_ * 8 + x_ * 2 + c_, "narrow": z_ * 2 + yh_}

    def rows(i, size):
        return pl.ds(pl.multiple_of(i * size, size), size)

    def send(src, dst, t, group, to):
        pltpu.make_async_remote_copy(
            src_ref=src, dst_ref=dst, send_sem=send_sem.at[t, group],
            recv_sem=recv_sem.at[t, group], device_id=to, device_id_type=MESH,
        ).start()

    def wait(ref, sem):
        pltpu.make_async_copy(ref, ref, sem).wait()

    def add(refs):
        total = refs[0].astype(F32)
        for ref in refs[1:]:
            total = total + ref.astype(F32)
        return total

    def far_first(i):
        return jnp.where(i == 7, 0, jnp.where(i % 2 == 0, 4 + i // 2, 3 - i // 2))

    barrier = pltpu.get_barrier_semaphore()

    def greet(to):
        pl.semaphore_signal(barrier, inc=1, device_id=to, device_id_type=MESH)

    def greet_ring(i, carry):
        zz = (z + far_first(i)) % 8
        for h in range(2):
            greet(dev(oyl, x, c, zz, h))
            greet(dev(oyl, flip(x, 1), c, zz, h))
        return carry

    pltpu.make_async_copy(r_hbm, r_v, in_sem.at[0]).start()
    for i in range(NCH):
        part = pl.ds(i * CH, CH)
        pltpu.make_async_copy(b_hbm.at[part], b_v.at[part], in_sem.at[1 + i]).start()
    for i in range(NCH):
        part = pl.ds(i * CH, CH)
        pltpu.make_async_copy(l_hbm.at[part], l_v.at[part], in_sem.at[1 + NCH + i]).start()

    lax.fori_loop(0, 8, greet_ring, 0)

    def greet_line(i, carry):
        greet(dev(yl, x, c, (z + 1 + i) % 8, yh))
        return carry

    lax.fori_loop(0, 7, greet_line, 0)
    for h in range(2):
        for cc in range(2):
            greet(dev(oyl, flip(x, 2), cc, z, h))
            greet(dev(oyl, flip(flip(x, 1), 2), cc, z, h))
        greet(dev(oyl, x, 1 - c, z, h))
        greet(dev(oyl, flip(x, 1), 1 - c, z, h))
    greet(dev(yl, x, 1 - c, z, yh))

    def contract(lhs, cols, total):
        def step(k, carry):
            part = rows(k, BIG)
            p = lax.dot_general(
                lhs[part, cols], b_v[part, :], (((0,), (0,)), ((), ())),
                preferred_element_type=F32,
            )
            total[...] = jnp.where(k == 0, p, total[...] + p)
            return carry

        lax.fori_loop(0, NBIG, step, 0)

    def scatter(t):
        def convert(k):
            proj[t, k] = pacc[:, k * RANK:(k + 1) * RANK].astype(BF16)

        convert(6)
        convert(7)
        if t == 0:
            for k in (5, 4, 3, 2, 1, 0):
                convert(k)
            pl.semaphore_wait(barrier, PEERS)

        def across(i, carry):
            xx = (x + 2 + i) % 4
            for cc in range(2):
                for h in range(2):
                    send(
                        proj.at[t, pl.ds(6, 2), rows(xx * 4 + cc * 2 + h, 16)], p1.at[t, plane],
                        t, P1, dev(oyl, xx, cc, z, h),
                    )
            return carry

        lax.fori_loop(0, 4, across, 0)
        if t > 0:
            convert(4)
            convert(5)

        def ring(i, carry):
            zz = (z + far_first(i)) % 8
            for h in range(2):
                send(
                    proj.at[t, pl.ds(4, 2), rows(zz * 2 + h, 16)], rh.at[t, n],
                    t, RH, dev(oyl, x, c, zz, h),
                )
            return carry

        lax.fori_loop(0, 8, ring, 0)
        if t > 0:
            for k in (3, 2, 1, 0):
                convert(k)
        for a in range(4):
            zz = (1 - z // 4) * 4 + (z + a) % 4
            for h in range(2):
                send(
                    proj.at[t, 3, rows((zz % 4) * 2 + h, 32)],
                    r3.at[t, (z % 4) * 2 + yh], t, R3, dev(oyl, x, c, zz, h),
                )
        for a in range(2):
            zz = (flip(z, 2) // 2) * 2 + (z + a) % 2
            for h in range(2):
                send(
                    proj.at[t, 2, rows((zz % 2) * 2 + h, 64)],
                    r2.at[t, (z % 2) * 2 + yh], t, R2, dev(oyl, x, c, zz, h),
                )
        for h in range(2):
            send(
                proj.at[t, 1, pl.ds(h * 128, 128)], r1.at[t, yh],
                t, R1, dev(oyl, x, c, flip(z, 1), h),
            )
        for h in range(2):
            send(proj.at[t, 0, pl.ds(h * 128, 128)], r0.at[t, yh], t, R0, dev(oyl, x, c, z, h))

    def own_plane(t):
        wait(p1.at[t], recv_sem.at[t, P1])
        qp[t, 0] = add([p1[t, i, 0] for i in range(8)]).astype(BF16)
        qp[t, 1] = add([p1[t, i, 0] for i in range(8, 16)]).astype(BF16)
        qp[t, 2] = add([p1[t, i, 1] for i in range(16)]).astype(BF16)

        def line(i, carry):
            dz = far_first(i)
            zz = (z + dz) % 8
            send(qp.at[t, pl.ds(0, 2)], w6.at[t, dz - 1], t, P6, dev(yl, x, c, zz, yh))
            send(qp.at[t, 2], w7.at[t, dz], t, P7, dev(oyl, x, c, zz, yh))
            return carry

        lax.fori_loop(0, 7, line, 0)
        send(qp.at[t, 2], w7.at[t, 0], t, P7, dev(oyl, x, c, z, yh))

    def own_line(t):
        wait(w6.at[t], recv_sem.at[t, P6])
        for j in range(2):
            tp[t, 1 - j, 0] = add([qp[t, j]] + [w6[t, i, j] for i in range(7)]).astype(BF16)
        wait(w7.at[t], recv_sem.at[t, P7])
        top = add([w7[t, i] for i in range(8)]).astype(BF16)
        tp[t, 0, 1] = top
        tp[t, 1, 1] = top

        def across(i, carry):
            xx = (x + 2 + i) % 4
            for cc in range(2):
                for h in range(2):
                    send(
                        tp.at[t, xx // 2], sib.at[t, pl.ds(6, 2), rows(plane, 16)],
                        t, S67, dev(oyl, xx, cc, z, h),
                    )
            return carry

        lax.fori_loop(0, 4, across, 0)

    def own_ring(t):
        wait(rh.at[t], recv_sem.at[t, RH])
        for k in range(2):
            q45[t, k] = add([rh[t, i, k] for i in range(16)])
        send(q45.at[t], d5.at[t], t, D5, dev(yl, x, 1 - c, z, yh))

    def own_pair(t):
        wait(d5.at[t], recv_sem.at[t, D5])
        t5[t] = (q45[t, 1] + d5[t, 1]).astype(BF16)
        t4[t] = d5[t, 0].astype(BF16)

        def ring(i, carry):
            zz = (z + far_first(i)) % 8
            for h in range(2):
                send(t5.at[t], sib.at[t, 5, rows(n, 16)], t, S5, dev(oyl, flip(x, 1), c, zz, h))
                send(t4.at[t], sib.at[t, 4, rows(n, 16)], t, S4, dev(oyl, x, c, zz, h))
            return carry

        lax.fori_loop(0, 8, ring, 0)

    def own_0(t):
        wait(r0.at[t], recv_sem.at[t, R0])
        for h in range(2):
            send(r0.at[t, 1 - h], sib.at[t, 0, rows(yh, 128)], t, S0, dev(oyl, x, c, z, h))

    def own_1(t):
        wait(r1.at[t], recv_sem.at[t, R1])
        q1[t] = add([r1[t, 0], r1[t, 1]]).astype(BF16)
        for h in range(2):
            send(q1.at[t], sib.at[t, 1, rows(yh, 128)], t, S1, dev(oyl, x, c, z, h))

    def own_2(t):
        wait(r2.at[t], recv_sem.at[t, R2])
        q2[t] = add([r2[t, i] for i in range(4)]).astype(BF16)
        for a in range(2):
            zz = (z // 2) * 2 + (z + 1 + a) % 2
            for h in range(2):
                send(q2.at[t], sib.at[t, 2, rows((z % 2) * 2 + yh, 64)], t, S2, dev(oyl, x, c, zz, h))

    def own_3(t):
        wait(r3.at[t], recv_sem.at[t, R3])
        q3[t] = add([r3[t, i] for i in range(8)]).astype(BF16)
        for a in range(4):
            zz = (z // 4) * 4 + (z + 2 + a) % 4
            for h in range(2):
                send(q3.at[t], sib.at[t, 3, rows((z % 4) * 2 + yh, 32)], t, S3, dev(oyl, x, c, zz, h))

    def arrive(t, groups):
        for k, count, s in groups:
            ref = sib.at[t, k] if count == 1 else sib.at[t, pl.ds(k, count)]
            wait(ref, recv_sem.at[t, s])

    def turn(t, levels):
        for k in levels:
            st[k * RANK:(k + 1) * RANK, :] = sib[t, k].T

    LOW = ((0, 1, S0), (1, 1, S1), (2, 1, S2), (3, 1, S3))

    def gram_block(i):
        contract(b_v, pl.ds(i * 256, 256), gacc)
        gram[pl.ds(i * 256, 256), :] = (GAIN * gacc[...]).astype(BF16)

    def through_gram(pair):
        both = jnp.concatenate([sib[0, 2 * pair], sib[0, 2 * pair + 1]], axis=1)
        pacc[...] -= jnp.dot(
            both, gram[pl.ds(pair * 256, 256), :], preferred_element_type=F32
        )

    wait(r_v, in_sem.at[0])
    d_v[...] = (r_v[...].astype(F32) / CENTRE).astype(BF16)
    for k in range(NCH):
        part = pl.ds(k * CH, CH)
        wait(b_v.at[part], in_sem.at[1 + k])
        p = lax.dot_general(
            d_v[part, :], b_v[part, :], (((0,), (0,)), ((), ())), preferred_element_type=F32
        )
        pacc[...] = p if k == 0 else pacc[...] + p
    scatter(0)
    for k in range(NCH):
        part = pl.ds(k * CH, CH)
        wait(l_v.at[part], in_sem.at[1 + NCH + k])

    def leaf_0(k, carry):
        part = rows(k, BIG)
        first = r_v[part, :].astype(F32)
        rest = first - jnp.dot(l_v[part, :], d_v[...], preferred_element_type=F32)
        acc_v[part, :] = rest
        u_v[part, :] = (KEEP * (first / CENTRE) + GAIN * rest).astype(BF16)
        return carry

    lax.fori_loop(0, NBIG, leaf_0, 0)
    contract(u_v, slice(None), pacc)
    gram_block(0)
    own_plane(0)
    own_ring(0)
    own_pair(0)
    own_3(0)
    own_2(0)
    own_1(0)
    own_0(0)
    gram_block(1)
    own_line(0)
    gram_block(2)
    gram_block(3)
    arrive(0, LOW)
    through_gram(0)
    through_gram(1)
    arrive(0, ((4, 1, S4), (5, 1, S5)))
    through_gram(2)
    arrive(0, ((6, 2, S67),))
    through_gram(3)
    scatter(1)

    turn(0, range(LEVELS))

    def middle(k, carry):
        part = rows(k, BIG)
        rest = acc_v[part, :] - jnp.dot(b_v[part, :], st[...], preferred_element_type=F32)
        d0 = r_v[part, :].astype(F32) / CENTRE
        d1 = KEEP * d0 + GAIN * rest
        acc_v[part, :] = rest
        x_v[part, :] = d0 + d1
        d_v[part, :] = d1.astype(BF16)
        return carry

    lax.fori_loop(0, NBIG, middle, 0)

    def leaf_1(k, carry):
        part = rows(k, BIG)
        acc_v[part, :] -= jnp.dot(l_v[part, :], d_v[...], preferred_element_type=F32)
        return carry

    lax.fori_loop(0, NBIG, leaf_1, 0)
    own_plane(1)
    own_ring(1)
    own_pair(1)
    own_3(1)
    own_2(1)
    own_1(1)
    own_0(1)
    own_line(1)
    arrive(1, LOW)
    turn(1, range(4))

    def expand_low(k, carry):
        part = rows(k, BIG)
        acc_v[part, :] -= jnp.dot(
            b_v[part, 0:HIGH], st[0:HIGH, :], preferred_element_type=F32
        )
        return carry

    lax.fori_loop(0, NBIG, expand_low, 0)

    for t in range(ITERS):
        for k, s in ((0, S0), (0, R0), (1, R1), (2, R2), (3, R3), (1, S1), (2, S2), (3, S3), (4, S4), (5, S5)):
            wait(proj.at[t, k], send_sem.at[t, s])
        wait(proj.at[t, pl.ds(4, 2)], send_sem.at[t, RH])
        wait(proj.at[t, pl.ds(6, 2)], send_sem.at[t, P1])
        wait(proj.at[t, pl.ds(6, 2)], send_sem.at[t, S67])
        wait(w6.at[t], send_sem.at[t, P6])
        wait(w7.at[t], send_sem.at[t, P7])
        wait(d5.at[t], send_sem.at[t, D5])
    arrive(1, ((4, 1, S4), (5, 1, S5)))
    turn(1, (4, 5))
    arrive(1, ((6, 2, S67),))
    turn(1, (6, 7))


def finish(acc_v, x_v, b_v, st, x_hbm, o_hbm, o_v, sem):
    copies = [pltpu.make_async_copy(x_v, x_hbm, sem.at[0])]
    copies[0].start()
    for k in range(NCH):
        part = pl.ds(k * CH, CH)
        o_v[part, :] = acc_v[part, :] - jnp.dot(
            b_v[part, HIGH:], st[HIGH:, :], preferred_element_type=F32
        )
        copies.append(pltpu.make_async_copy(o_v.at[part], o_hbm.at[part], sem.at[1 + k]))
        copies[-1].start()
    for copy in copies:
        copy.wait()


def on_device(right_side, leaf_blocks, level_bases):
    hbm = pl.BlockSpec(memory_space=pltpu.HBM)
    vmem = pl.BlockSpec(memory_space=pltpu.VMEM)
    field = jax.ShapeDtypeStruct((LEAF, VECS), F32)
    state = pl.pallas_call(
        kernel,
        out_shape=(
            field, field, jax.ShapeDtypeStruct((LEAF, COLS), BF16),
            jax.ShapeDtypeStruct((COLS, VECS), BF16),
        ),
        in_specs=[hbm] * 3,
        out_specs=(vmem,) * 4,
        scratch_shapes=[
            pltpu.VMEM((LEAF, VECS), BF16),
            pltpu.VMEM((LEAF, LEAF), BF16),
            pltpu.VMEM((LEAF, VECS), BF16),
            pltpu.VMEM((LEAF, VECS), BF16),
            pltpu.VMEM((VECS, COLS), F32),
            pltpu.VMEM((VECS, COLS), F32),
            pltpu.VMEM((COLS, COLS), BF16),
            pltpu.VMEM((ITERS, LEVELS, VECS, RANK), BF16),
            pltpu.VMEM((ITERS, LEVELS, VECS, RANK), BF16),
            pltpu.VMEM((ITERS, 2, 128, RANK), BF16),
            pltpu.VMEM((ITERS, 2, 128, RANK), BF16),
            pltpu.VMEM((ITERS, 4, 64, RANK), BF16),
            pltpu.VMEM((ITERS, 8, 32, RANK), BF16),
            pltpu.VMEM((ITERS, 16, 2, 16, RANK), BF16),
            pltpu.VMEM((ITERS, 2, 16, RANK), F32),
            pltpu.VMEM((ITERS, 16, 2, 16, RANK), BF16),
            pltpu.VMEM((ITERS, 7, 2, 16, RANK), BF16),
            pltpu.VMEM((ITERS, 8, 16, RANK), BF16),
            pltpu.VMEM((ITERS, 128, RANK), BF16),
            pltpu.VMEM((ITERS, 64, RANK), BF16),
            pltpu.VMEM((ITERS, 32, RANK), BF16),
            pltpu.VMEM((ITERS, 2, 16, RANK), F32),
            pltpu.VMEM((ITERS, 16, RANK), BF16),
            pltpu.VMEM((ITERS, 16, RANK), BF16),
            pltpu.VMEM((ITERS, 3, 16, RANK), BF16),
            pltpu.VMEM((ITERS, 2, 2, 16, RANK), BF16),
            pltpu.SemaphoreType.DMA((1 + 2 * NCH,)),
            pltpu.SemaphoreType.DMA((ITERS, 16)),
            pltpu.SemaphoreType.DMA((ITERS, 16)),
        ],
        compiler_params=pltpu.CompilerParams(
            collective_id=0, has_side_effects=True, vmem_limit_bytes=40 * 1024 * 1024
        ),
        name="chebyshev",
    )(*(pltpu.with_memory_space_constraint(v, pltpu.HBM) for v in (right_side, leaf_blocks, level_bases)))
    return pl.pallas_call(
        finish,
        out_shape=(field, field),
        in_specs=[vmem] * 4,
        out_specs=(hbm, hbm),
        scratch_shapes=[
            pltpu.VMEM((LEAF, VECS), F32),
            pltpu.SemaphoreType.DMA((1 + NCH,)),
        ],
        compiler_params=pltpu.CompilerParams(vmem_limit_bytes=16 * 1024 * 1024),
        name="finish",
    )(*state)


def solution(mesh):
    return jax.shard_map(
        on_device,
        mesh=mesh,
        in_specs=(P(("wide", "narrow"), None),) * 3,
        out_specs=(P(("wide", "narrow"), None),) * 2,
        check_vma=False,
    )
```

time: 65.7 us -> 52.1 us (0.79)
  Pallas kernels: 61.5 us -> 51.4 us
  local copies, waits for them, and re-layouts: 3.41 us -> 0 us
    pallas_call x1 -> x2, Pallas kernels: 61.5 us -> 51.4 us  [the longest x1 49.6 us: on_device(): pl.pallas_call(kernel, out_shape=(field, field, jax.ShapeDtypeStruct((LEA...]
    unnamed x4 -> x0, local copies, waits for them, and re-layouts: 3.41 us -> none
where the time goes in v2:
time: 52.1 us; the launch traced here: 52 us
  Pallas kernels  51.4 us (99%)
  between operations  0.64 us (1%)
    pallas_call x1, Pallas kernels, on_device(): pl.pallas_call(kernel, out_shape=(field, field, jax.ShapeDtypeStruct((LEA...  49.6 us
    pallas_call x1, Pallas kernels, on_device(): pl.pallas_call(finish, out_shape=(field, field), in_specs=[vmem] * 4, out...  1.72 us

profile of v2, /device:TPU:1, one launch (start us, length us, event | category | flops | bytes accessed | tf_op | source)
XLA Modules:
  0.0 52.0 jit_solution(4311286005615064066)
XLA Ops:
  0.6 49.6 %chebyshev.1 = (f32[1536,256]{1,0:T(8,128)S(1)}, f32[1536,256]{1,0:T(8,128)S(1)}, bf16[1536,1024]{1,0:T(8,128)(2,1)S(1)}, bf16[1024,256]{1,0:T(8,128)(2,1)S(1)}) custom-call(bf16[1536,256]{1,0:T(8,128)(2,1)} %r_hbm.1, bf16[1536,1536]{1,0:T(8,128)(2,1)} %l_hbm.1, bf16[1536,1024]{1,0:T(8,128)(2,1)} %b_hbm.1), custom_call_target="tpu_custom_call" | custom-call | tf_op jit(solution)/shard_map/chebyshev/pallas_call | solution.py:399
  50.3 1.7 %finish.1 = (f32[1536,256]{1,0:T(8,128)}, f32[1536,256]{1,0:T(8,128)}) custom-call(f32[1536,256]{1,0:T(8,128)S(1)} %get-tuple-element.6.acc_v, f32[1536,256]{1,0:T(8,128)S(1)} %get-tuple-element.7.x_v, bf16[1536,1024]{1,0:T(8,128)(2,1)S(1)} %get-tuple-element.8.b_v, bf16[1024,256]{1,0:T(8,128)(2,1)S(1)} %get-tuple-element.9.st), custom_call_target="tpu_custom_call" | custom-call | tf_op jit(solution)/shard_map/finish/pallas_call | solution.py:443

commit v3 on v2

--- a/solution.py
+++ b/solution.py
@@ -19,7 +19,7 @@
 Q0 = 1.0 / SIGMA
 Q1 = 1.0 / (2.0 * SIGMA - Q0)
 KEEP, GAIN = Q1 * Q0, 2.0 * Q1 / HALF
-S0, S1, S2, S3, S4, S5, S67, R0, R1, R2, R3, RH, D5, P1, P6, P7 = range(16)
+S0, S1, S2, S3, S4, S5, S67, R0, R1, R2, R3, RH, D5, F5, P1, P6, P7 = range(17)
 PEERS = 52
 
 
@@ -78,13 +78,16 @@
         return carry
 
     pltpu.make_async_copy(r_hbm, r_v, in_sem.at[0]).start()
-    for i in range(NCH):
-        part = pl.ds(i * CH, CH)
-        pltpu.make_async_copy(b_hbm.at[part], b_v.at[part], in_sem.at[1 + i]).start()
-    for i in range(NCH):
-        part = pl.ds(i * CH, CH)
-        pltpu.make_async_copy(l_hbm.at[part], l_v.at[part], in_sem.at[1 + NCH + i]).start()
-
+
+    def load_bases(side):
+        cols = pl.ds((1 - side) * HIGH, HIGH)
+        for i in range(NCH):
+            part = pl.ds(i * CH, CH)
+            pltpu.make_async_copy(
+                b_hbm.at[part, cols], b_v.at[part, cols], in_sem.at[1 + side * NCH + i]
+            ).start()
+
+    load_bases(0)
     lax.fori_loop(0, 8, greet_ring, 0)
 
     def greet_line(i, carry):
@@ -99,6 +102,10 @@
         greet(dev(oyl, x, 1 - c, z, h))
         greet(dev(oyl, flip(x, 1), 1 - c, z, h))
     greet(dev(yl, x, 1 - c, z, yh))
+    load_bases(1)
+    for i in range(NCH):
+        part = pl.ds(i * CH, CH)
+        pltpu.make_async_copy(l_hbm.at[part], l_v.at[part], in_sem.at[1 + 2 * NCH + i]).start()
 
     def contract(lhs, cols, total):
         def step(k, carry):
@@ -112,17 +119,11 @@
 
         lax.fori_loop(0, NBIG, step, 0)
 
-    def scatter(t):
-        def convert(k):
+    def convert(t, levels):
+        for k in levels:
             proj[t, k] = pacc[:, k * RANK:(k + 1) * RANK].astype(BF16)
 
-        convert(6)
-        convert(7)
-        if t == 0:
-            for k in (5, 4, 3, 2, 1, 0):
-                convert(k)
-            pl.semaphore_wait(barrier, PEERS)
-
+    def scatter_67(t):
         def across(i, carry):
             xx = (x + 2 + i) % 4
             for cc in range(2):
@@ -134,23 +135,20 @@
             return carry
 
         lax.fori_loop(0, 4, across, 0)
-        if t > 0:
-            convert(4)
-            convert(5)
-
+
+    def scatter_45(t):
         def ring(i, carry):
             zz = (z + far_first(i)) % 8
             for h in range(2):
                 send(
-                    proj.at[t, pl.ds(4, 2), rows(zz * 2 + h, 16)], rh.at[t, n],
+                    proj.at[t, pl.ds(4, 2), rows(h * 8 + zz, 16)], rh.at[t, n],
                     t, RH, dev(oyl, x, c, zz, h),
                 )
             return carry
 
         lax.fori_loop(0, 8, ring, 0)
-        if t > 0:
-            for k in (3, 2, 1, 0):
-                convert(k)
+
+    def scatter_3(t):
         for a in range(4):
             zz = (1 - z // 4) * 4 + (z + a) % 4
             for h in range(2):
@@ -158,6 +156,8 @@
                     proj.at[t, 3, rows((zz % 4) * 2 + h, 32)],
                     r3.at[t, (z % 4) * 2 + yh], t, R3, dev(oyl, x, c, zz, h),
                 )
+
+    def scatter_low(t):
         for a in range(2):
             zz = (flip(z, 2) // 2) * 2 + (z + a) % 2
             for h in range(2):
@@ -221,14 +221,34 @@
         t5[t] = (q45[t, 1] + d5[t, 1]).astype(BF16)
         t4[t] = d5[t, 0].astype(BF16)
 
+        @pl.when(yh == c)
+        def _():
+            def ring(i, carry):
+                zz = (z + far_first(i)) % 8
+                for h in range(2):
+                    send(
+                        t5.at[t], sib.at[t, 5, rows(yh * 8 + z, 16)],
+                        t, S5, dev(oyl, flip(x, 1), c, zz, h),
+                    )
+                return carry
+
+            lax.fori_loop(0, 8, ring, 0)
+
         def ring(i, carry):
             zz = (z + far_first(i)) % 8
             for h in range(2):
-                send(t5.at[t], sib.at[t, 5, rows(n, 16)], t, S5, dev(oyl, flip(x, 1), c, zz, h))
-                send(t4.at[t], sib.at[t, 4, rows(n, 16)], t, S4, dev(oyl, x, c, zz, h))
+                send(t4.at[t], sib.at[t, 4, rows(yh * 8 + z, 16)], t, S4, dev(oyl, x, c, zz, h))
             return carry
 
         lax.fori_loop(0, 8, ring, 0)
+
+    def pass_on(t):
+        half = sib.at[t, 5, rows(c, 128)]
+        wait(half, recv_sem.at[t, S5])
+        send(half, half, t, F5, dev(yl, x, 1 - c, z, yh))
+
+    def other_half(t):
+        wait(sib.at[t, 5, rows(1 - c, 128)], recv_sem.at[t, F5])
 
     def own_0(t):
         wait(r0.at[t], recv_sem.at[t, R0])
@@ -272,25 +292,39 @@
         contract(b_v, pl.ds(i * 256, 256), gacc)
         gram[pl.ds(i * 256, 256), :] = (GAIN * gacc[...]).astype(BF16)
 
-    def through_gram(pair):
+    def through_gram(pair, first=0, last=LEVELS):
         both = jnp.concatenate([sib[0, 2 * pair], sib[0, 2 * pair + 1]], axis=1)
-        pacc[...] -= jnp.dot(
-            both, gram[pl.ds(pair * 256, 256), :], preferred_element_type=F32
+        cols = slice(first * RANK, last * RANK)
+        pacc[:, cols] -= jnp.dot(
+            both, gram[pl.ds(pair * 256, 256), cols], preferred_element_type=F32
         )
 
     wait(r_v, in_sem.at[0])
     d_v[...] = (r_v[...].astype(F32) / CENTRE).astype(BF16)
+
+    def project(side):
+        cols = pl.ds((1 - side) * HIGH, HIGH)
+        for k in range(NCH):
+            part = pl.ds(k * CH, CH)
+            wait(b_v.at[part, cols], in_sem.at[1 + side * NCH + k])
+            p = lax.dot_general(
+                d_v[part, :], b_v[part, cols], (((0,), (0,)), ((), ())),
+                preferred_element_type=F32,
+            )
+            pacc[:, cols] = p if k == 0 else pacc[:, cols] + p
+
+    project(0)
+    convert(0, (7, 6, 5, 4))
+    pl.semaphore_wait(barrier, PEERS)
+    scatter_67(0)
+    scatter_45(0)
+    project(1)
+    convert(0, (3, 2, 1, 0))
+    scatter_3(0)
+    scatter_low(0)
     for k in range(NCH):
         part = pl.ds(k * CH, CH)
-        wait(b_v.at[part], in_sem.at[1 + k])
-        p = lax.dot_general(
-            d_v[part, :], b_v[part, :], (((0,), (0,)), ((), ())), preferred_element_type=F32
-        )
-        pacc[...] = p if k == 0 else pacc[...] + p
-    scatter(0)
-    for k in range(NCH):
-        part = pl.ds(k * CH, CH)
-        wait(l_v.at[part], in_sem.at[1 + NCH + k])
+        wait(l_v.at[part], in_sem.at[1 + 2 * NCH + k])
 
     def leaf_0(k, carry):
         part = rows(k, BIG)
@@ -314,14 +348,24 @@
     own_line(0)
     gram_block(2)
     gram_block(3)
+    pass_on(0)
     arrive(0, LOW)
     through_gram(0)
     through_gram(1)
-    arrive(0, ((4, 1, S4), (5, 1, S5)))
+    arrive(0, ((4, 1, S4),))
+    other_half(0)
     through_gram(2)
     arrive(0, ((6, 2, S67),))
-    through_gram(3)
-    scatter(1)
+    through_gram(3, 6, 8)
+    convert(1, (6, 7))
+    scatter_67(1)
+    through_gram(3, 4, 6)
+    convert(1, (4, 5))
+    scatter_45(1)
+    through_gram(3, 0, 4)
+    convert(1, (3, 2, 1, 0))
+    scatter_3(1)
+    scatter_low(1)
 
     turn(0, range(LEVELS))
 
@@ -351,6 +395,7 @@
     own_1(1)
     own_0(1)
     own_line(1)
+    pass_on(1)
     arrive(1, LOW)
     turn(1, range(4))
 
@@ -364,15 +409,22 @@
     lax.fori_loop(0, NBIG, expand_low, 0)
 
     for t in range(ITERS):
-        for k, s in ((0, S0), (0, R0), (1, R1), (2, R2), (3, R3), (1, S1), (2, S2), (3, S3), (4, S4), (5, S5)):
+        for k, s in ((0, S0), (0, R0), (1, R1), (2, R2), (3, R3), (1, S1), (2, S2), (3, S3), (4, S4)):
             wait(proj.at[t, k], send_sem.at[t, s])
+
+        @pl.when(yh == c)
+        def _():
+            wait(proj.at[t, 5], send_sem.at[t, S5])
+
+        wait(r0.at[t, 0], send_sem.at[t, F5])
         wait(proj.at[t, pl.ds(4, 2)], send_sem.at[t, RH])
         wait(proj.at[t, pl.ds(6, 2)], send_sem.at[t, P1])
         wait(proj.at[t, pl.ds(6, 2)], send_sem.at[t, S67])
         wait(w6.at[t], send_sem.at[t, P6])
         wait(w7.at[t], send_sem.at[t, P7])
         wait(d5.at[t], send_sem.at[t, D5])
-    arrive(1, ((4, 1, S4), (5, 1, S5)))
+    arrive(1, ((4, 1, S4),))
+    other_half(1)
     turn(1, (4, 5))
     arrive(1, ((6, 2, S67),))
     turn(1, (6, 7))
@@ -431,9 +483,9 @@
             pltpu.VMEM((ITERS, 16, RANK), BF16),
             pltpu.VMEM((ITERS, 3, 16, RANK), BF16),
             pltpu.VMEM((ITERS, 2, 2, 16, RANK), BF16),
-            pltpu.SemaphoreType.DMA((1 + 2 * NCH,)),
-            pltpu.SemaphoreType.DMA((ITERS, 16)),
-            pltpu.SemaphoreType.DMA((ITERS, 16)),
+            pltpu.SemaphoreType.DMA((1 + 3 * NCH,)),
+            pltpu.SemaphoreType.DMA((ITERS, 17)),
+            pltpu.SemaphoreType.DMA((ITERS, 17)),
         ],
         compiler_params=pltpu.CompilerParams(
             collective_id=0, has_side_effects=True, vmem_limit_bytes=40 * 1024 * 1024

time: 52.1 us -> 51.9 us (level)
  no operation moved by 1% of the time
where the time goes in v3:
time: 51.9 us; the launch traced here: 51.8 us
  Pallas kernels  51.2 us (99%)
  between operations  0.64 us (1%)
    pallas_call x1, Pallas kernels, on_device(): pl.pallas_call(kernel, out_shape=(field, field, jax.ShapeDtypeStruct((LEA...  49.4 us
    pallas_call x1, Pallas kernels, on_device(): pl.pallas_call(finish, out_shape=(field, field), in_specs=[vmem] * 4, out...  1.72 us

profile of v3, /device:TPU:1, one launch (start us, length us, event | category | flops | bytes accessed | tf_op | source)
XLA Modules:
  0.0 51.8 jit_solution(2015705582518345907)
XLA Ops:
  0.6 49.4 %chebyshev.1 = (f32[1536,256]{1,0:T(8,128)S(1)}, f32[1536,256]{1,0:T(8,128)S(1)}, bf16[1536,1024]{1,0:T(8,128)(2,1)S(1)}, bf16[1024,256]{1,0:T(8,128)(2,1)S(1)}) custom-call(bf16[1536,256]{1,0:T(8,128)(2,1)} %r_hbm.1, bf16[1536,1536]{1,0:T(8,128)(2,1)} %l_hbm.1, bf16[1536,1024]{1,0:T(8,128)(2,1)} %b_hbm.1), custom_call_target="tpu_custom_call" | custom-call | tf_op jit(solution)/shard_map/chebyshev/pallas_call | solution.py:451
  50.1 1.7 %finish.1 = (f32[1536,256]{1,0:T(8,128)}, f32[1536,256]{1,0:T(8,128)}) custom-call(f32[1536,256]{1,0:T(8,128)S(1)} %get-tuple-element.6.acc_v, f32[1536,256]{1,0:T(8,128)S(1)} %get-tuple-element.7.x_v, bf16[1536,1024]{1,0:T(8,128)(2,1)S(1)} %get-tuple-element.8.b_v, bf16[1024,256]{1,0:T(8,128)(2,1)S(1)} %get-tuple-element.9.st), custom_call_target="tpu_custom_call" | custom-call | tf_op jit(solution)/shard_map/finish/pallas_call | solution.py:495
